TPU v7x, 512 devices: a 8x2x16 block of a 8x16x16 slice. The times are simulated.
512 devices in a mesh: parts: 2 (over y), blk: 16 (over z), sub: 8 (over x), rep: 2 (over core).
Axes of the slice: x: 8, y: 2, z: 16, core: 2. Of those that a mesh axis runs over, the one named last changes fastest.
The devices are a block of a 8x16x16 slice.
Arguments:
- queries: bfloat16 [2048, 32, 128], P(('parts', 'blk', 'sub', 'rep')), parts along dimension 0, may hold values from -1.5 to 1.5
- passages: bfloat16 [2048, 128, 128], P(('parts', 'blk')), parts along dimension 0, may hold values from -1.5 to 1.5
- lengths: int32 [2048], P(('parts', 'blk')), parts along dimension 0, may hold values from 8 to 128
- slot_of: int32 [2048], P('parts'), parts along dimension 0, may hold values from 0 to 1023, each once
- candidates: int32 [2048, 256], P(('parts', 'blk', 'sub', 'rep')), parts along dimension 0, may hold values from 0 to 1023
Outputs:
- score: float32 [2048, 256], P(('parts', 'blk', 'sub', 'rep')), parts along dimension 0
- top: float32 [2048, 10], P(('parts', 'blk', 'sub', 'rep')), parts along dimension 0
There are 2 independent parts, one for each index of `parts`. A program takes and returns all parts, laid end to end along the dimension named above; each array names one. Nothing has to cross between parts.
Inputs may be any that keep to these rules, and one draw needn't show every extreme that they name: `slot_of`: a permutation; storage row r lies on the blk index r // 64. `candidates`: passage ids, repeats allowed. `lengths`: the live slots of a row are its first ones.
All inputs are finite; a program needn't handle non-finite values.
Results may differ from a plain program's by a relative error of at most 0.0003.
Values may be sent and summed in bfloat16 or wider, within the bound.
A program may use at most 64 MiB of HBM per device.

v0:
```python
import jax
import jax.numpy as jnp
from jax import lax
from jax.sharding import PartitionSpec as P

TOPN = 10


def score_table(rows_q, passages, lengths):
    queries_here = rows_q.shape[0]
    tokens = rows_q.shape[1]
    width = rows_q.shape[2]
    count = passages.shape[0]
    span = passages.shape[1]
    group = 4
    flat = rows_q.reshape(queries_here * tokens, width)
    blocks = passages.reshape(count // group, group * span, width)
    spans = lengths.reshape(count // group, group)

    def one_block(pair):
        piece, live_count = pair
        similar = lax.dot_general(
            flat, piece, (((1,), (1,)), ((), ())), preferred_element_type=jnp.float32
        )
        similar = similar.reshape(queries_here * tokens, group, span)
        live = lax.broadcasted_iota(jnp.int32, (group, span), 1) < live_count[:, None]
        best = jnp.max(jnp.where(live[None], similar, -1e30), axis=2)
        return jnp.sum(best.reshape(queries_here, tokens, group), axis=1) / tokens

    table = lax.map(one_block, (blocks, spans))
    return jnp.transpose(table, (1, 0, 2)).reshape(queries_here, count)


def shards(queries, passages, lengths, slot_of, candidates):
    table = score_table(lax.all_gather(queries, "blk", axis=0, tiled=True), passages, lengths)
    whole = lax.all_to_all(table, "blk", split_axis=0, concat_axis=1, tiled=True)
    score = jnp.take_along_axis(whole, jnp.take(slot_of, candidates, axis=0), axis=1)
    top = lax.top_k(score, TOPN)[0]
    return (score, top)


def solution(mesh):
    return jax.shard_map(
        shards,
        mesh=mesh,
        in_specs=(
            P(("parts", "blk", "sub", "rep"), None, None),
            P(("parts", "blk"), None, None),
            P(("parts", "blk")),
            P("parts"),
            P(("parts", "blk", "sub", "rep"), None),
        ),
        out_specs=(
            P(("parts", "blk", "sub", "rep"), None),
            P(("parts", "blk", "sub", "rep"), None),
        ),
        check_vma=False,
    )
```

profile of v0, /device:TPU:86, one launch (start us, length us, event | category | flops | bytes accessed | tf_op | source)
XLA Modules:
  0.0 134.1 jit_solution(3773919563160055687)
XLA Ops:
  0.7 0.7 reshape.67
  1.4 71.3 %all_gather.3 = bf16[64,32,128]{2,1,0:T(8,128)(2,1)S(1)} all-gather(bf16[4,32,128]{2,1,0:T(8,128)(2,1)} %param.7), channel_id=1, replica_groups=mesh['parts'=2,'blk'=16,'sub'=8,'rep'=2] {'blk'}, dimensions={0}, use_global_device_ids=true | all-gather | bytes 557056 | tf_op jit(solution)/shard_map/all_gather | solution.py:35
  72.6 31.7 %while.10 = (s32[]{:T(128)}, f32[16,64,4]{1,2,0:T(4,128)S(1)}, s32[16,4]{1,0:T(8,128)S(1)}, bf16[16,512,128]{2,1,0:T(8,128)(2,1)}, bf16[2048,128]{1,0:T(8,128)(2,1)S(1)}, /*index=5*/s32[]{:T(128)}, f32[]{:T(128)}) while((s32[]{:T(128)}, f32[16,64,4]{1,2,0:T(4,128)S(1)}, s32[16,4]{1,0:T(8,128)S(1)}, bf16[16,512,128]{2,1,0:T(8,128)(2,1)}, ...), condition=%wide.region_3.4_spmd, body=%wide.region_0.3_spmd.sunk | while | flops 270533120 | bytes 792725 | solution.py:30
  72.7 1.7 %select_reduce_fusion.2 = f32[2048,4]{0,1:T(4,128)S(1)} fusion(pred[4,128]{1,0:T(4,128)(4,1)S(1)} %iota_compare_fusion.2, bf16[2048,128]{1,0:T(8,128)(2,1)S(1)} %get-tuple-element.93, bf16[16,512,128]{2,1,0:T(8,128)(2,1)} %get-tuple-element.92, s32[]{:T(128)S(6)} %copy.19), kind=kOutput, calls=%fused_computation.2.clone.1 | convolution fusion | flops 270524416 | bytes 688644 | tf_op jit(solution)/shard_map/while/body/eval_jaxpr/dot_general | solution.py:22
  74.7 1.6 %select_reduce_fusion.2 = f32[2048,4]{0,1:T(4,128)S(1)} fusion(pred[4,128]{1,0:T(4,128)(4,1)S(1)} %iota_compare_fusion.2, bf16[2048,128]{1,0:T(8,128)(2,1)S(1)} %get-tuple-element.93, bf16[16,512,128]{2,1,0:T(8,128)(2,1)} %get-tuple-element.92, s32[]{:T(128)S(6)} %copy.19), kind=kOutput, calls=%fused_computation.2.clone.1 | convolution fusion | flops 270524416 | bytes 688644 | tf_op jit(solution)/shard_map/while/body/eval_jaxpr/dot_general | solution.py:22
  76.7 1.6 %select_reduce_fusion.2 = f32[2048,4]{0,1:T(4,128)S(1)} fusion(pred[4,128]{1,0:T(4,128)(4,1)S(1)} %iota_compare_fusion.2, bf16[2048,128]{1,0:T(8,128)(2,1)S(1)} %get-tuple-element.93, bf16[16,512,128]{2,1,0:T(8,128)(2,1)} %get-tuple-element.92, s32[]{:T(128)S(6)} %copy.19), kind=kOutput, calls=%fused_computation.2.clone.1 | convolution fusion | flops 270524416 | bytes 688644 | tf_op jit(solution)/shard_map/while/body/eval_jaxpr/dot_general | solution.py:22
  78.7 1.6 %select_reduce_fusion.2 = f32[2048,4]{0,1:T(4,128)S(1)} fusion(pred[4,128]{1,0:T(4,128)(4,1)S(1)} %iota_compare_fusion.2, bf16[2048,128]{1,0:T(8,128)(2,1)S(1)} %get-tuple-element.93, bf16[16,512,128]{2,1,0:T(8,128)(2,1)} %get-tuple-element.92, s32[]{:T(128)S(6)} %copy.19), kind=kOutput, calls=%fused_computation.2.clone.1 | convolution fusion | flops 270524416 | bytes 688644 | tf_op jit(solution)/shard_map/while/body/eval_jaxpr/dot_general | solution.py:22
  80.7 1.6 %select_reduce_fusion.2 = f32[2048,4]{0,1:T(4,128)S(1)} fusion(pred[4,128]{1,0:T(4,128)(4,1)S(1)} %iota_compare_fusion.2, bf16[2048,128]{1,0:T(8,128)(2,1)S(1)} %get-tuple-element.93, bf16[16,512,128]{2,1,0:T(8,128)(2,1)} %get-tuple-element.92, s32[]{:T(128)S(6)} %copy.19), kind=kOutput, calls=%fused_computation.2.clone.1 | convolution fusion | flops 270524416 | bytes 688644 | tf_op jit(solution)/shard_map/while/body/eval_jaxpr/dot_general | solution.py:22
  82.6 1.6 %select_reduce_fusion.2 = f32[2048,4]{0,1:T(4,128)S(1)} fusion(pred[4,128]{1,0:T(4,128)(4,1)S(1)} %iota_compare_fusion.2, bf16[2048,128]{1,0:T(8,128)(2,1)S(1)} %get-tuple-element.93, bf16[16,512,128]{2,1,0:T(8,128)(2,1)} %get-tuple-element.92, s32[]{:T(128)S(6)} %copy.19), kind=kOutput, calls=%fused_computation.2.clone.1 | convolution fusion | flops 270524416 | bytes 688644 | tf_op jit(solution)/shard_map/while/body/eval_jaxpr/dot_general | solution.py:22
  84.6 1.6 %select_reduce_fusion.2 = f32[2048,4]{0,1:T(4,128)S(1)} fusion(pred[4,128]{1,0:T(4,128)(4,1)S(1)} %iota_compare_fusion.2, bf16[2048,128]{1,0:T(8,128)(2,1)S(1)} %get-tuple-element.93, bf16[16,512,128]{2,1,0:T(8,128)(2,1)} %get-tuple-element.92, s32[]{:T(128)S(6)} %copy.19), kind=kOutput, calls=%fused_computation.2.clone.1 | convolution fusion | flops 270524416 | bytes 688644 | tf_op jit(solution)/shard_map/while/body/eval_jaxpr/dot_general | solution.py:22
  86.6 1.6 %select_reduce_fusion.2 = f32[2048,4]{0,1:T(4,128)S(1)} fusion(pred[4,128]{1,0:T(4,128)(4,1)S(1)} %iota_compare_fusion.2, bf16[2048,128]{1,0:T(8,128)(2,1)S(1)} %get-tuple-element.93, bf16[16,512,128]{2,1,0:T(8,128)(2,1)} %get-tuple-element.92, s32[]{:T(128)S(6)} %copy.19), kind=kOutput, calls=%fused_computation.2.clone.1 | convolution fusion | flops 270524416 | bytes 688644 | tf_op jit(solution)/shard_map/while/body/eval_jaxpr/dot_general | solution.py:22
  88.6 1.6 %select_reduce_fusion.2 = f32[2048,4]{0,1:T(4,128)S(1)} fusion(pred[4,128]{1,0:T(4,128)(4,1)S(1)} %iota_compare_fusion.2, bf16[2048,128]{1,0:T(8,128)(2,1)S(1)} %get-tuple-element.93, bf16[16,512,128]{2,1,0:T(8,128)(2,1)} %get-tuple-element.92, s32[]{:T(128)S(6)} %copy.19), kind=kOutput, calls=%fused_computation.2.clone.1 | convolution fusion | flops 270524416 | bytes 688644 | tf_op jit(solution)/shard_map/while/body/eval_jaxpr/dot_general | solution.py:22
  90.6 1.6 %select_reduce_fusion.2 = f32[2048,4]{0,1:T(4,128)S(1)} fusion(pred[4,128]{1,0:T(4,128)(4,1)S(1)} %iota_compare_fusion.2, bf16[2048,128]{1,0:T(8,128)(2,1)S(1)} %get-tuple-element.93, bf16[16,512,128]{2,1,0:T(8,128)(2,1)} %get-tuple-element.92, s32[]{:T(128)S(6)} %copy.19), kind=kOutput, calls=%fused_computation.2.clone.1 | convolution fusion | flops 270524416 | bytes 688644 | tf_op jit(solution)/shard_map/while/body/eval_jaxpr/dot_general | solution.py:22
  92.5 1.6 %select_reduce_fusion.2 = f32[2048,4]{0,1:T(4,128)S(1)} fusion(pred[4,128]{1,0:T(4,128)(4,1)S(1)} %iota_compare_fusion.2, bf16[2048,128]{1,0:T(8,128)(2,1)S(1)} %get-tuple-element.93, bf16[16,512,128]{2,1,0:T(8,128)(2,1)} %get-tuple-element.92, s32[]{:T(128)S(6)} %copy.19), kind=kOutput, calls=%fused_computation.2.clone.1 | convolution fusion | flops 270524416 | bytes 688644 | tf_op jit(solution)/shard_map/while/body/eval_jaxpr/dot_general | solution.py:22
  94.5 1.6 %select_reduce_fusion.2 = f32[2048,4]{0,1:T(4,128)S(1)} fusion(pred[4,128]{1,0:T(4,128)(4,1)S(1)} %iota_compare_fusion.2, bf16[2048,128]{1,0:T(8,128)(2,1)S(1)} %get-tuple-element.93, bf16[16,512,128]{2,1,0:T(8,128)(2,1)} %get-tuple-element.92, s32[]{:T(128)S(6)} %copy.19), kind=kOutput, calls=%fused_computation.2.clone.1 | convolution fusion | flops 270524416 | bytes 688644 | tf_op jit(solution)/shard_map/while/body/eval_jaxpr/dot_general | solution.py:22
  96.5 1.6 %select_reduce_fusion.2 = f32[2048,4]{0,1:T(4,128)S(1)} fusion(pred[4,128]{1,0:T(4,128)(4,1)S(1)} %iota_compare_fusion.2, bf16[2048,128]{1,0:T(8,128)(2,1)S(1)} %get-tuple-element.93, bf16[16,512,128]{2,1,0:T(8,128)(2,1)} %get-tuple-element.92, s32[]{:T(128)S(6)} %copy.19), kind=kOutput, calls=%fused_computation.2.clone.1 | convolution fusion | flops 270524416 | bytes 688644 | tf_op jit(solution)/shard_map/while/body/eval_jaxpr/dot_general | solution.py:22
  98.5 1.6 %select_reduce_fusion.2 = f32[2048,4]{0,1:T(4,128)S(1)} fusion(pred[4,128]{1,0:T(4,128)(4,1)S(1)} %iota_compare_fusion.2, bf16[2048,128]{1,0:T(8,128)(2,1)S(1)} %get-tuple-element.93, bf16[16,512,128]{2,1,0:T(8,128)(2,1)} %get-tuple-element.92, s32[]{:T(128)S(6)} %copy.19), kind=kOutput, calls=%fused_computation.2.clone.1 | convolution fusion | flops 270524416 | bytes 688644 | tf_op jit(solution)/shard_map/while/body/eval_jaxpr/dot_general | solution.py:22
  100.5 1.6 %select_reduce_fusion.2 = f32[2048,4]{0,1:T(4,128)S(1)} fusion(pred[4,128]{1,0:T(4,128)(4,1)S(1)} %iota_compare_fusion.2, bf16[2048,128]{1,0:T(8,128)(2,1)S(1)} %get-tuple-element.93, bf16[16,512,128]{2,1,0:T(8,128)(2,1)} %get-tuple-element.92, s32[]{:T(128)S(6)} %copy.19), kind=kOutput, calls=%fused_computation.2.clone.1 | convolution fusion | flops 270524416 | bytes 688644 | tf_op jit(solution)/shard_map/while/body/eval_jaxpr/dot_general | solution.py:22
  102.4 1.6 %select_reduce_fusion.2 = f32[2048,4]{0,1:T(4,128)S(1)} fusion(pred[4,128]{1,0:T(4,128)(4,1)S(1)} %iota_compare_fusion.2, bf16[2048,128]{1,0:T(8,128)(2,1)S(1)} %get-tuple-element.93, bf16[16,512,128]{2,1,0:T(8,128)(2,1)} %get-tuple-element.92, s32[]{:T(128)S(6)} %copy.19), kind=kOutput, calls=%fused_computation.2.clone.1 | convolution fusion | flops 270524416 | bytes 688644 | tf_op jit(solution)/shard_map/while/body/eval_jaxpr/dot_general | solution.py:22
  105.6 3.9 %all-to-all-start = ((f32[16,1,256]{2,1,0:T(1,128)}), f32[16,1,256]{2,1,0:T(1,128)S(1)}, u32[]{:S(2)}, u32[]{:S(2)}) async-start(f32[16,1,256]{2,1,0:T(1,128)} %reshape.92), calls=%async_computation | async-start | bytes 32768 | tf_op jit(solution)/shard_map/all_to_all | solution.py:36
  109.6 4.5 %gather_fusion = s32[1024]{0:T(1024)S(1)} fusion(s32[1024]{0:T(1024)S(1)} %copy-done, s32[1024]{0:T(1024)S(1)} %broadcast_clamp_fusion), kind=kCustom, calls=%fused_computation | custom fusion | bytes 12288 | tf_op jit(solution)/shard_map/jit(_take)/gather | solution.py:37
  114.2 7.5 %all-to-all-done = f32[16,1,256]{2,1,0:T(1,128)S(1)} async-done(((f32[16,1,256]{2,1,0:T(1,128)}), f32[16,1,256]{2,1,0:T(1,128)S(1)}, u32[]{:S(2)}, u32[]{:S(2)}) %all-to-all-start) | async-done | bytes 16416 | tf_op jit(solution)/shard_map/all_to_all | solution.py:36
  123.0 9.1 %gather_fusion.1 = f32[1024]{0:T(1024)S(1)} fusion(f32[4,1024]{1,0:T(4,128)S(1)} %all_to_all.17, s32[1024]{0:T(1024)S(1)} %bitcast.43), kind=kCustom, calls=%fused_computation.1 | custom fusion | bytes 16384 | tf_op jit(solution)/shard_map/jit(take_along_axis)/gather | solution.py:37
  132.2 1.9 %sort_prefixfusion = f32[4,10]{1,0:T(4,128)} fusion(f32[4,256]{1,0:T(4,128)S(1)} %and_select_fusion), kind=kCustom, calls=%top_k.9.sort_prefix | custom fusion | flops 10240 | bytes 4256 | tf_op jit(solution)/shard_map/top_k | solution.py:38
  (103 shorter events, 7.6 us)
Async XLA Ops:
  0.6 109.0 %copy-start = (s32[1024]{0:T(1024)S(1)}, s32[1024]{0:T(1024)}, u32[]{:S(2)}) copy-start(s32[1024]{0:T(1024)} %param.10) | copy-start | bytes 12292
  72.6 36.9 %copy-start.1 = (s32[4,256]{1,0:T(4,128)S(1)}, s32[4,256]{1,0:T(4,128)}, u32[]{:S(2)}) copy-start(s32[4,256]{1,0:T(4,128)} %param.11) | copy-start | bytes 12292
  105.6 16.0 %all-to-all-start = ((f32[16,1,256]{2,1,0:T(1,128)}), f32[16,1,256]{2,1,0:T(1,128)S(1)}, u32[]{:S(2)}, u32[]{:S(2)}) async-start(f32[16,1,256]{2,1,0:T(1,128)} %reshape.92), calls=%async_computation | async-start | bytes 32768 | tf_op jit(solution)/shard_map/all_to_all | solution.py:36
  132.2 1.9 %copy-start.2 = (f32[4,256]{1,0:T(4,128)}, f32[4,256]{1,0:T(4,128)S(1)}, u32[]{:S(2)}) copy-start(f32[4,256]{1,0:T(4,128)S(1)} %and_select_fusion) | copy-start | bytes 12292
where the time goes:
time: 135 us; the launch traced here: 134 us
  blocking collectives  71.3 us (53%)
  matrix products  26.2 us (19%)
  local copies, waits for them, and re-layouts  18.1 us (13%)
  waiting for transfers between devices  7.45 us (6%)
  other arithmetic  5.8 us (4%)
  starting transfers between devices  3.93 us (3%)
    all_gather x1, blocking collectives, shards(): lax.all_gather(queries, 'blk', axis=0, tiled=True)  71.3 us
    dot_general x16, matrix products, one_block(): lax.dot_general(flat, piece, (((1,), (1,)), ((), ())), preferred_element_...  26.2 us
    gather x2, local copies, waits for them, and re-layouts, shards(): jnp.take_along_axis(whole, jnp.take(slot_of, candidates, axis=0), axis=1)  9.13 us
    all_to_all x1, waiting for transfers between devices, shards(): lax.all_to_all(table, 'blk', split_axis=0, concat_axis=1, tiled=True)  7.45 us
    gather x2, local copies, waits for them, and re-layouts, shards(): jnp.take(slot_of, candidates, axis=0)  4.54 us
    all_to_all x1, starting transfers between devices, shards(): lax.all_to_all(table, 'blk', split_axis=0, concat_axis=1, tiled=True)  3.93 us
  transfers between devices with their start and end apart: 1, of which 1 were waited for; matrix products, arithmetic and copies ran while one was open for 3% of the time, Pallas kernels for 0%

commit v1 on v0

--- a/solution.py
+++ b/solution.py
@@ -4,6 +4,14 @@
 from jax.sharding import PartitionSpec as P
 
 TOPN = 10
+
+
+def deliver_group(sheet, comm_axis):
+    latest = lax.axis_size(comm_axis)
+    oldest = jnp.stack([sheet] * latest, axis=0)
+    current_value = lax.all_to_all(oldest, comm_axis, split_axis=0, concat_axis=0)
+    finding = jnp.concatenate(current_value, 0)
+    return finding
 
 
 def score_table(rows_q, passages, lengths):
@@ -32,7 +40,7 @@
 
 
 def shards(queries, passages, lengths, slot_of, candidates):
-    table = score_table(lax.all_gather(queries, "blk", axis=0, tiled=True), passages, lengths)
+    table = score_table(deliver_group(queries, "blk"), passages, lengths)
     whole = lax.all_to_all(table, "blk", split_axis=0, concat_axis=1, tiled=True)
     score = jnp.take_along_axis(whole, jnp.take(slot_of, candidates, axis=0), axis=1)
     top = lax.top_k(score, TOPN)[0]

time: 135 us -> 140 us (1.037)
  the two profiles are of different devices: /device:TPU:86 before, /device:TPU:70 now
where the time goes in v1:
time: 140 us; the launch traced here: 139 us
  starting transfers between devices  50.3 us (36%)
  waiting for transfers between devices  35.8 us (26%)
  matrix products  26.2 us (19%)
  local copies, waits for them, and re-layouts  19.1 us (14%)
  other arithmetic  6.5 us (5%)
    all_to_all x1, starting transfers between devices, deliver_group(): lax.all_to_all(oldest, comm_axis, split_axis=0, concat_axis=0)  43.7 us
    dot_general x16, matrix products, one_block(): lax.dot_general(flat, piece, (((1,), (1,)), ((), ())), preferred_element_...  26.2 us
    all_to_all x1, waiting for transfers between devices, deliver_group(): lax.all_to_all(oldest, comm_axis, split_axis=0, concat_axis=0)  23.5 us
    all_to_all x1, waiting for transfers between devices, shards(): lax.all_to_all(table, 'blk', split_axis=0, concat_axis=1, tiled=True)  12.3 us
    gather x2, local copies, waits for them, and re-layouts, shards(): jnp.take_along_axis(whole, jnp.take(slot_of, candidates, axis=0), axis=1)  9.13 us
    all_to_all x1, starting transfers between devices, shards(): lax.all_to_all(table, 'blk', split_axis=0, concat_axis=1, tiled=True)  6.58 us
    gather x2, local copies, waits for them, and re-layouts, shards(): jnp.take(slot_of, candidates, axis=0)  4.54 us
  transfers between devices with their start and end apart: 2, of which 2 were waited for; matrix products, arithmetic and copies ran while one was open for 4% of the time, Pallas kernels for 0%

profile of v1, /device:TPU:70, one launch (start us, length us, event | category | flops | bytes accessed | tf_op | source)
XLA Modules:
  0.0 139.2 jit_solution(6780456601556637360)
XLA Ops:
  0.6 1.7 %stack.2 = bf16[16,4,32,128]{3,2,1,0:T(8,128)(2,1)} broadcast(bf16[4,32,128]{2,1,0:T(8,128)(2,1)} %param.7), dimensions={1,2,3} | broadcast | bytes 557056 | tf_op jit(solution)/shard_map/stack | solution.py:11
  2.3 43.7 %all-to-all-start = ((bf16[16,4,32,128]{3,2,1,0:T(8,128)(2,1)}), bf16[16,4,32,128]{3,2,1,0:T(8,128)(2,1)S(1)}, u32[]{:S(2)}, u32[]{:S(2)}) async-start(bf16[16,4,32,128]{3,2,1,0:T(8,128)(2,1)} %stack.2), calls=%async_computation | async-start | bytes 1048576 | tf_op jit(solution)/shard_map/all_to_all | solution.py:12
  46.7 4.5 %gather_fusion = s32[1024]{0:T(1024)S(1)} fusion(s32[1024]{0:T(1024)S(1)} %copy-done, s32[1024]{0:T(1024)S(1)} %broadcast_clamp_fusion), kind=kCustom, calls=%fused_computation | custom fusion | bytes 12288 | tf_op jit(solution)/shard_map/jit(_take)/gather | solution.py:45
  51.4 23.5 %all-to-all-done = bf16[16,4,32,128]{3,2,1,0:T(8,128)(2,1)S(1)} async-done(((bf16[16,4,32,128]{3,2,1,0:T(8,128)(2,1)}), bf16[16,4,32,128]{3,2,1,0:T(8,128)(2,1)S(1)}, u32[]{:S(2)}, u32[]{:S(2)}) %all-to-all-start) | async-done | bytes 524320 | tf_op jit(solution)/shard_map/all_to_all | solution.py:12
  74.9 31.6 %while.10 = (s32[]{:T(128)}, f32[16,64,4]{1,2,0:T(4,128)S(1)}, s32[16,4]{1,0:T(8,128)S(1)}, bf16[16,512,128]{2,1,0:T(8,128)(2,1)}, bf16[2048,128]{1,0:T(8,128)(2,1)S(1)}, /*index=5*/s32[]{:T(128)}, f32[]{:T(128)}) while((s32[]{:T(128)}, f32[16,64,4]{1,2,0:T(4,128)S(1)}, s32[16,4]{1,0:T(8,128)S(1)}, bf16[16,512,128]{2,1,0:T(8,128)(2,1)}, ...), condition=%wide.region_3.4_spmd, body=%wide.region_0.3_spmd.sunk | while | flops 270533120 | bytes 793225 | solution.py:38
  75.0 1.6 %select_reduce_fusion.2 = f32[2048,4]{0,1:T(4,128)S(1)} fusion(pred[4,128]{1,0:T(4,128)(4,1)S(1)} %iota_compare_fusion.2, bf16[2048,128]{1,0:T(8,128)(2,1)S(1)} %get-tuple-element.93, bf16[16,512,128]{2,1,0:T(8,128)(2,1)} %get-tuple-element.92, s32[]{:T(128)} %get-tuple-element.82), kind=kOutput, calls=%fused_computation.2.clone.1 | convolution fusion | flops 270524416 | bytes 689152 | tf_op jit(solution)/shard_map/while/body/eval_jaxpr/dot_general | solution.py:30
  77.0 1.6 %select_reduce_fusion.2 = f32[2048,4]{0,1:T(4,128)S(1)} fusion(pred[4,128]{1,0:T(4,128)(4,1)S(1)} %iota_compare_fusion.2, bf16[2048,128]{1,0:T(8,128)(2,1)S(1)} %get-tuple-element.93, bf16[16,512,128]{2,1,0:T(8,128)(2,1)} %get-tuple-element.92, s32[]{:T(128)} %get-tuple-element.82), kind=kOutput, calls=%fused_computation.2.clone.1 | convolution fusion | flops 270524416 | bytes 689152 | tf_op jit(solution)/shard_map/while/body/eval_jaxpr/dot_general | solution.py:30
  78.9 1.6 %select_reduce_fusion.2 = f32[2048,4]{0,1:T(4,128)S(1)} fusion(pred[4,128]{1,0:T(4,128)(4,1)S(1)} %iota_compare_fusion.2, bf16[2048,128]{1,0:T(8,128)(2,1)S(1)} %get-tuple-element.93, bf16[16,512,128]{2,1,0:T(8,128)(2,1)} %get-tuple-element.92, s32[]{:T(128)} %get-tuple-element.82), kind=kOutput, calls=%fused_computation.2.clone.1 | convolution fusion | flops 270524416 | bytes 689152 | tf_op jit(solution)/shard_map/while/body/eval_jaxpr/dot_general | solution.py:30
  80.9 1.6 %select_reduce_fusion.2 = f32[2048,4]{0,1:T(4,128)S(1)} fusion(pred[4,128]{1,0:T(4,128)(4,1)S(1)} %iota_compare_fusion.2, bf16[2048,128]{1,0:T(8,128)(2,1)S(1)} %get-tuple-element.93, bf16[16,512,128]{2,1,0:T(8,128)(2,1)} %get-tuple-element.92, s32[]{:T(128)} %get-tuple-element.82), kind=kOutput, calls=%fused_computation.2.clone.1 | convolution fusion | flops 270524416 | bytes 689152 | tf_op jit(solution)/shard_map/while/body/eval_jaxpr/dot_general | solution.py:30
  82.9 1.6 %select_reduce_fusion.2 = f32[2048,4]{0,1:T(4,128)S(1)} fusion(pred[4,128]{1,0:T(4,128)(4,1)S(1)} %iota_compare_fusion.2, bf16[2048,128]{1,0:T(8,128)(2,1)S(1)} %get-tuple-element.93, bf16[16,512,128]{2,1,0:T(8,128)(2,1)} %get-tuple-element.92, s32[]{:T(128)} %get-tuple-element.82), kind=kOutput, calls=%fused_computation.2.clone.1 | convolution fusion | flops 270524416 | bytes 689152 | tf_op jit(solution)/shard_map/while/body/eval_jaxpr/dot_general | solution.py:30
  84.9 1.6 %select_reduce_fusion.2 = f32[2048,4]{0,1:T(4,128)S(1)} fusion(pred[4,128]{1,0:T(4,128)(4,1)S(1)} %iota_compare_fusion.2, bf16[2048,128]{1,0:T(8,128)(2,1)S(1)} %get-tuple-element.93, bf16[16,512,128]{2,1,0:T(8,128)(2,1)} %get-tuple-element.92, s32[]{:T(128)} %get-tuple-element.82), kind=kOutput, calls=%fused_computation.2.clone.1 | convolution fusion | flops 270524416 | bytes 689152 | tf_op jit(solution)/shard_map/while/body/eval_jaxpr/dot_general | solution.py:30
  86.8 1.6 %select_reduce_fusion.2 = f32[2048,4]{0,1:T(4,128)S(1)} fusion(pred[4,128]{1,0:T(4,128)(4,1)S(1)} %iota_compare_fusion.2, bf16[2048,128]{1,0:T(8,128)(2,1)S(1)} %get-tuple-element.93, bf16[16,512,128]{2,1,0:T(8,128)(2,1)} %get-tuple-element.92, s32[]{:T(128)} %get-tuple-element.82), kind=kOutput, calls=%fused_computation.2.clone.1 | convolution fusion | flops 270524416 | bytes 689152 | tf_op jit(solution)/shard_map/while/body/eval_jaxpr/dot_general | solution.py:30
  88.8 1.6 %select_reduce_fusion.2 = f32[2048,4]{0,1:T(4,128)S(1)} fusion(pred[4,128]{1,0:T(4,128)(4,1)S(1)} %iota_compare_fusion.2, bf16[2048,128]{1,0:T(8,128)(2,1)S(1)} %get-tuple-element.93, bf16[16,512,128]{2,1,0:T(8,128)(2,1)} %get-tuple-element.92, s32[]{:T(128)} %get-tuple-element.82), kind=kOutput, calls=%fused_computation.2.clone.1 | convolution fusion | flops 270524416 | bytes 689152 | tf_op jit(solution)/shard_map/while/body/eval_jaxpr/dot_general | solution.py:30
  92.8 1.6 %select_reduce_fusion.2 = f32[2048,4]{0,1:T(4,128)S(1)} fusion(pred[4,128]{1,0:T(4,128)(4,1)S(1)} %iota_compare_fusion.2, bf16[2048,128]{1,0:T(8,128)(2,1)S(1)} %get-tuple-element.93, bf16[16,512,128]{2,1,0:T(8,128)(2,1)} %get-tuple-element.92, s32[]{:T(128)} %get-tuple-element.82), kind=kOutput, calls=%fused_computation.2.clone.1 | convolution fusion | flops 270524416 | bytes 689152 | tf_op jit(solution)/shard_map/while/body/eval_jaxpr/dot_general | solution.py:30
  94.8 1.6 %select_reduce_fusion.2 = f32[2048,4]{0,1:T(4,128)S(1)} fusion(pred[4,128]{1,0:T(4,128)(4,1)S(1)} %iota_compare_fusion.2, bf16[2048,128]{1,0:T(8,128)(2,1)S(1)} %get-tuple-element.93, bf16[16,512,128]{2,1,0:T(8,128)(2,1)} %get-tuple-element.92, s32[]{:T(128)} %get-tuple-element.82), kind=kOutput, calls=%fused_computation.2.clone.1 | convolution fusion | flops 270524416 | bytes 689152 | tf_op jit(solution)/shard_map/while/body/eval_jaxpr/dot_general | solution.py:30
  96.7 1.6 %select_reduce_fusion.2 = f32[2048,4]{0,1:T(4,128)S(1)} fusion(pred[4,128]{1,0:T(4,128)(4,1)S(1)} %iota_compare_fusion.2, bf16[2048,128]{1,0:T(8,128)(2,1)S(1)} %get-tuple-element.93, bf16[16,512,128]{2,1,0:T(8,128)(2,1)} %get-tuple-element.92, s32[]{:T(128)} %get-tuple-element.82), kind=kOutput, calls=%fused_computation.2.clone.1 | convolution fusion | flops 270524416 | bytes 689152 | tf_op jit(solution)/shard_map/while/body/eval_jaxpr/dot_general | solution.py:30
  98.7 1.6 %select_reduce_fusion.2 = f32[2048,4]{0,1:T(4,128)S(1)} fusion(pred[4,128]{1,0:T(4,128)(4,1)S(1)} %iota_compare_fusion.2, bf16[2048,128]{1,0:T(8,128)(2,1)S(1)} %get-tuple-element.93, bf16[16,512,128]{2,1,0:T(8,128)(2,1)} %get-tuple-element.92, s32[]{:T(128)} %get-tuple-element.82), kind=kOutput, calls=%fused_computation.2.clone.1 | convolution fusion | flops 270524416 | bytes 689152 | tf_op jit(solution)/shard_map/while/body/eval_jaxpr/dot_general | solution.py:30
  100.7 1.6 %select_reduce_fusion.2 = f32[2048,4]{0,1:T(4,128)S(1)} fusion(pred[4,128]{1,0:T(4,128)(4,1)S(1)} %iota_compare_fusion.2, bf16[2048,128]{1,0:T(8,128)(2,1)S(1)} %get-tuple-element.93, bf16[16,512,128]{2,1,0:T(8,128)(2,1)} %get-tuple-element.92, s32[]{:T(128)} %get-tuple-element.82), kind=kOutput, calls=%fused_computation.2.clone.1 | convolution fusion | flops 270524416 | bytes 689152 | tf_op jit(solution)/shard_map/while/body/eval_jaxpr/dot_general | solution.py:30
  102.7 1.6 %select_reduce_fusion.2 = f32[2048,4]{0,1:T(4,128)S(1)} fusion(pred[4,128]{1,0:T(4,128)(4,1)S(1)} %iota_compare_fusion.2, bf16[2048,128]{1,0:T(8,128)(2,1)S(1)} %get-tuple-element.93, bf16[16,512,128]{2,1,0:T(8,128)(2,1)} %get-tuple-element.92, s32[]{:T(128)} %get-tuple-element.82), kind=kOutput, calls=%fused_computation.2.clone.1 | convolution fusion | flops 270524416 | bytes 689152 | tf_op jit(solution)/shard_map/while/body/eval_jaxpr/dot_general | solution.py:30
  104.7 1.6 %select_reduce_fusion.2 = f32[2048,4]{0,1:T(4,128)S(1)} fusion(pred[4,128]{1,0:T(4,128)(4,1)S(1)} %iota_compare_fusion.2, bf16[2048,128]{1,0:T(8,128)(2,1)S(1)} %get-tuple-element.93, bf16[16,512,128]{2,1,0:T(8,128)(2,1)} %get-tuple-element.92, s32[]{:T(128)} %get-tuple-element.82), kind=kOutput, calls=%fused_computation.2.clone.1 | convolution fusion | flops 270524416 | bytes 689152 | tf_op jit(solution)/shard_map/while/body/eval_jaxpr/dot_general | solution.py:30
  107.8 6.6 %all-to-all-start.1 = ((f32[16,1,256]{2,1,0:T(1,128)}), f32[16,1,256]{2,1,0:T(1,128)S(1)}, u32[]{:S(2)}, u32[]{:S(2)}) async-start(f32[16,1,256]{2,1,0:T(1,128)} %reshape.90), calls=%async_computation.1 | async-start | bytes 32768 | tf_op jit(solution)/shard_map/all_to_all | solution.py:44
  114.5 12.3 %all-to-all-done.1 = f32[16,1,256]{2,1,0:T(1,128)S(1)} async-done(((f32[16,1,256]{2,1,0:T(1,128)}), f32[16,1,256]{2,1,0:T(1,128)S(1)}, u32[]{:S(2)}, u32[]{:S(2)}) %all-to-all-start.1) | async-done | bytes 16416 | tf_op jit(solution)/shard_map/all_to_all | solution.py:44
  128.1 9.1 %gather_fusion.1 = f32[1024]{0:T(1024)S(1)} fusion(f32[4,1024]{1,0:T(4,128)S(1)} %all_to_all.21, s32[1024]{0:T(1024)S(1)} %bitcast.43), kind=kCustom, calls=%fused_computation.1 | custom fusion | bytes 16384 | tf_op jit(solution)/shard_map/jit(take_along_axis)/gather | solution.py:45
  137.3 1.9 %sort_prefixfusion = f32[4,10]{1,0:T(4,128)} fusion(f32[4,256]{1,0:T(4,128)S(1)} %and_select_fusion), kind=kCustom, calls=%top_k.9.sort_prefix | custom fusion | flops 10240 | bytes 4256 | tf_op jit(solution)/shard_map/top_k | solution.py:46
  (107 shorter events, 10.0 us)
Async XLA Ops:
  0.6 46.1 %copy-start = (s32[1024]{0:T(1024)S(1)}, s32[1024]{0:T(1024)}, u32[]{:S(2)}) copy-start(s32[1024]{0:T(1024)} %param.10) | copy-start | bytes 12292
  2.3 72.6 %all-to-all-start = ((bf16[16,4,32,128]{3,2,1,0:T(8,128)(2,1)}), bf16[16,4,32,128]{3,2,1,0:T(8,128)(2,1)S(1)}, u32[]{:S(2)}, u32[]{:S(2)}) async-start(bf16[16,4,32,128]{3,2,1,0:T(8,128)(2,1)} %stack.2), calls=%async_computation | async-start | bytes 1048576 | tf_op jit(solution)/shard_map/all_to_all | solution.py:12
  46.7 4.6 %copy-start.3 = (s32[64]{0:T(128)S(1)}, s32[64]{0:T(128)}, u32[]{:S(2)}) copy-start(s32[64]{0:T(128)} %param.9) | copy-start | bytes 772
  74.9 39.5 %copy-start.1 = (s32[4,256]{1,0:T(4,128)S(1)}, s32[4,256]{1,0:T(4,128)}, u32[]{:S(2)}) copy-start(s32[4,256]{1,0:T(4,128)} %param.11) | copy-start | bytes 12292
  107.8 18.9 %all-to-all-start.1 = ((f32[16,1,256]{2,1,0:T(1,128)}), f32[16,1,256]{2,1,0:T(1,128)S(1)}, u32[]{:S(2)}, u32[]{:S(2)}) async-start(f32[16,1,256]{2,1,0:T(1,128)} %reshape.90), calls=%async_computation.1 | async-start | bytes 32768 | tf_op jit(solution)/shard_map/all_to_all | solution.py:44
  137.3 1.9 %copy-start.2 = (f32[4,256]{1,0:T(4,128)}, f32[4,256]{1,0:T(4,128)S(1)}, u32[]{:S(2)}) copy-start(f32[4,256]{1,0:T(4,128)S(1)} %and_select_fusion) | copy-start | bytes 12292
